TPU v7x, 32 devices: a whole 2x2x4 slice. The times are simulated.
32 devices in a mesh: section: 2 (over x), dp: 16 (over z, y, core).
Axes of the slice: x: 2, y: 2, z: 4, core: 2. Of those that a mesh axis runs over, the one named last changes fastest.
Arguments:
- inputs: bfloat16 [2048, 8192], P('dp', 'section'), may hold values from -6 to 6
- cotangent: bfloat16 [2048, 8192], P('dp', 'section'), may hold values from -6 to 6
- weights: bfloat16 [2, 64, 8192], P('section'), may hold values from -0.0625 to 0.0625
- momentum: bfloat16 [2, 16, 64, 8192], P('section', 'dp'), may hold values from -6 to 6
- keep_index: int32 [2, 16, 128, 32], P('section', 'dp'), may hold values from 0 to 4095, as said below
Outputs:
- momentum_out: bfloat16 [2, 16, 64, 8192], P('section', 'dp')
- update: bfloat16 [2, 16, 64, 8192], P('section', 'dp')
Inputs may be any that keep to these rules, and one draw needn't show every extreme that they name: `keep_index`: the 32 positions of one block of one replica and layer are all different.
All inputs are finite; a program needn't handle non-finite values.
Results may differ from a plain program's by a relative error of at most 0.0095.
Values may be sent and summed in bfloat16 or wider, within the bound.
A program may use at most 64 MiB of HBM per device.

v0:
```python
import math
import jax
import jax.numpy as jnp
from jax import lax
from jax.sharding import PartitionSpec as P

MICRO = 8
DECAY = 0.999


def from_behind(value, axis, steps):
    count = lax.axis_size(axis)
    leading, last = (max(0, -steps), min(count, count - steps))
    return lax.ppermute(value, axis, [(source, source + steps) for source in range(leading, last)])


def dct_basis(length):
    freq = jnp.arange(length, dtype=jnp.float32)[:, None]
    position = jnp.arange(length, dtype=jnp.float32)[None, :]
    dct_table = jnp.cos(math.pi * (position + 0.5) * freq / length) * math.sqrt(2.0 / length)
    return jnp.where(freq == 0, dct_table * math.sqrt(0.5), dct_table)


def forward_groups(field_in, dct_table):
    row_count, columns = field_in.shape
    blocks = field_in.reshape(row_count // 64, 64, columns // 64, 64)
    coeffs = jnp.einsum(
        "kn,anbm,jm->akbj", dct_table, blocks, dct_table, precision=lax.Precision.HIGHEST
    )
    return coeffs.reshape(-1)


def inverse_groups(flat_in, dct_table, row_count, columns):
    blocks = flat_in.reshape(row_count // 64, 64, columns // 64, 64)
    field_out = jnp.einsum(
        "kn,akbj,jm->anbm", dct_table, blocks, dct_table, precision=lax.Precision.HIGHEST
    )
    return field_out.reshape(row_count, columns)


def group_offsets(position, col_groups):
    group_id = jnp.arange(position.shape[0], dtype=jnp.int32)[:, None]
    return (
        group_id // col_groups * (4096 * col_groups)
        + position // 64 * (64 * col_groups)
        + group_id % col_groups * 64
        + position % 64
    )


def silu_slope(pre_act):
    sigma_h = jax.nn.sigmoid(pre_act)
    return sigma_h * (1.0 + pre_act * (1.0 - sigma_h))


def store_slot(saved, value, slot_clip, is_valid):
    previous = lax.dynamic_index_in_dim(saved, slot_clip, 0, keepdims=False)
    return lax.dynamic_update_index_in_dim(
        saved, jnp.where(is_valid, value, previous), slot_clip, 0
    )


def local(inputs, cotangent, weights, momentum, keep_index):
    sections = lax.axis_size("section")
    section_index = lax.axis_index("section")
    whole_inputs, whole_grads = (
        lax.all_gather(inputs, "section", axis=1, tiled=True),
        lax.all_gather(cotangent, "section", axis=1, tiled=True),
    )
    weight = weights[0]
    row_count, columns = weight.shape
    tok_dev = whole_inputs.shape[0]
    tok_mb = tok_dev // MICRO
    tick_count = MICRO + sections - 1
    first_in = whole_inputs.reshape(MICRO, tok_mb, columns)
    last_grad = whole_grads.reshape(MICRO, tok_mb, columns)

    def forward_tick(tick_idx, loop_state):
        incoming, saved_x, saved_a, saved_h = loop_state
        micro_slot = tick_idx - section_index
        is_valid = (micro_slot >= 0) & (micro_slot < MICRO)
        slot_clip = jnp.clip(micro_slot, 0, MICRO - 1)
        own_first = lax.dynamic_index_in_dim(first_in, slot_clip, 0, keepdims=False)
        activation = jnp.where(section_index == 0, own_first, incoming)
        pre_act = jnp.einsum("td,cd->tc", activation, weight, preferred_element_type=jnp.float32)
        gated_act = jax.nn.silu(pre_act).astype(jnp.bfloat16)
        result = (
            activation.astype(jnp.float32)
            + jnp.einsum("tc,cd->td", gated_act, weight, preferred_element_type=jnp.float32)
        ).astype(jnp.bfloat16)
        saved_x = store_slot(saved_x, activation, slot_clip, is_valid)
        saved_a = store_slot(saved_a, gated_act, slot_clip, is_valid)
        saved_h = store_slot(saved_h, pre_act, slot_clip, is_valid)
        outgoing = from_behind(result, "section", 1)
        return (outgoing, saved_x, saved_a, saved_h)

    start_state = (
        jnp.zeros((tok_mb, columns), jnp.bfloat16),
        jnp.zeros((MICRO, tok_mb, columns), jnp.bfloat16),
        jnp.zeros((MICRO, tok_mb, row_count), jnp.bfloat16),
        jnp.zeros((MICRO, tok_mb, row_count), jnp.float32),
    )
    loop_state = lax.fori_loop(0, tick_count, forward_tick, start_state)
    saved_x, saved_a, saved_h = (loop_state[1], loop_state[2], loop_state[3])

    def backward_tick(tick_idx, loop_state):
        incoming, saved_g, saved_d = loop_state
        micro_slot = tick_idx - (sections - 1 - section_index)
        is_valid = (micro_slot >= 0) & (micro_slot < MICRO)
        slot_clip = jnp.clip(micro_slot, 0, MICRO - 1)
        own_last = lax.dynamic_index_in_dim(last_grad, slot_clip, 0, keepdims=False)
        grad_in = jnp.where(section_index == sections - 1, own_last, incoming)
        pre_act = lax.dynamic_index_in_dim(saved_h, slot_clip, 0, keepdims=False)
        errors = jnp.einsum("td,cd->tc", grad_in, weight, preferred_element_type=jnp.float32)
        deltas = (errors * silu_slope(pre_act)).astype(jnp.bfloat16)
        saved_g = store_slot(saved_g, grad_in, slot_clip, is_valid)
        saved_d = store_slot(saved_d, deltas, slot_clip, is_valid)
        sent_back = (
            grad_in.astype(jnp.float32)
            + jnp.einsum("tc,cd->td", deltas, weight, preferred_element_type=jnp.float32)
        ).astype(jnp.bfloat16)
        outgoing = from_behind(sent_back, "section", -1)
        return (outgoing, saved_g, saved_d)

    back_state = (
        jnp.zeros((tok_mb, columns), jnp.bfloat16),
        jnp.zeros((MICRO, tok_mb, columns), jnp.bfloat16),
        jnp.zeros((MICRO, tok_mb, row_count), jnp.bfloat16),
    )
    back_out = lax.fori_loop(0, tick_count, backward_tick, back_state)
    saved_g = back_out[1].reshape(tok_dev, columns)
    saved_d = back_out[2].reshape(tok_dev, row_count)
    grad_total = jnp.einsum(
        "tc,td->cd",
        saved_a.reshape(tok_dev, row_count),
        saved_g,
        preferred_element_type=jnp.float32,
    )
    grad_total = grad_total + jnp.einsum(
        "tc,td->cd", saved_d, saved_x.reshape(tok_dev, columns), preferred_element_type=jnp.float32
    )
    dct_table = dct_basis(64)
    momentum_new = DECAY * momentum[0, 0].astype(jnp.float32) + grad_total
    coeffs = forward_groups(momentum_new, dct_table)
    offsets = group_offsets(keep_index[0, 0], columns // 64)
    kept_values = coeffs[offsets]
    own_sparse = jnp.zeros_like(coeffs).at[offsets.reshape(-1)].add(kept_values.reshape(-1))
    own_field = inverse_groups(own_sparse, dct_table, row_count, columns)
    momentum_out = (momentum_new - own_field).astype(jnp.bfloat16)
    update = lax.psum(own_field, "dp")
    return (momentum_out[None, None], update.astype(jnp.bfloat16)[None, None])


def solution(mesh):
    return jax.shard_map(
        local,
        mesh=mesh,
        in_specs=(
            P("dp", "section"),
            P("dp", "section"),
            P("section", None, None),
            P("section", "dp", None, None),
            P("section", "dp", None, None),
        ),
        out_specs=(P("section", "dp", None, None), P("section", "dp", None, None)),
        check_vma=False,
    )
```

profile of v0, /device:TPU:0, one launch (start us, length us, event | category | flops | bytes accessed | tf_op | source)
XLA Modules:
  0.0 467.1 jit_solution(12507494876444105098)
XLA Ops:
  10.7 34.7 %all-gather.3.cloned.1.call-done = bf16[128,8192]{1,0:T(8,128)(2,1)} async-done(((bf16[128,4096]{1,0:T(8,128)(2,1)}), bf16[128,8192]{1,0:T(8,128)(2,1)}) %all-gather.3.cloned.1.call-update) | async-done | bytes 2097168 | tf_op jit(solution)/shard_map/all_gather | solution.py:67
  46.3 116.0 %while.39 = (s32[]{:T(128)}, bf16[16,8192]{1,0:T(8,128)(2,1)}, bf16[8,16,8192]{2,1,0:T(8,128)(2,1)S(1)}, bf16[8,16,64]{2,1,0:T(8,128)(2,1)S(1)}, f32[8,16,64]{2,...) while((s32[]{:T(128)}, bf16[16,8192]{1,0:T(8,128)(2,1)}, ...), condition=%wide.region_1.2_spmd, body=%wide.region_0.1_spmd.sunk | while | flops 34222088 | bytes 6873366 | solution.py:103
  48.9 2.3 collective-permute-start
  51.3 8.7 %collective-permute-done = bf16[16,8192]{1,0:T(8,128)(2,1)S(1)} collective-permute-done((bf16[16,8192]{1,0:T(8,128)(2,1)}, bf16[16,8192]{1,0:T(8,128)(2,1)S(1)}, u32[]{:S(2)}, u32[]{:S(2)}) %collective-permute-start) | collective-permute-done | bytes 262176 | tf_op jit(solution)/shard_map/while/body/eval_jaxpr/ppermute | solution.py:14
  63.2 4.4 collective-permute-start
  67.6 11.2 %collective-permute-done = bf16[16,8192]{1,0:T(8,128)(2,1)S(1)} collective-permute-done((bf16[16,8192]{1,0:T(8,128)(2,1)}, bf16[16,8192]{1,0:T(8,128)(2,1)S(1)}, u32[]{:S(2)}, u32[]{:S(2)}) %collective-permute-start) | collective-permute-done | bytes 262176 | tf_op jit(solution)/shard_map/while/body/eval_jaxpr/ppermute | solution.py:14
  82.1 4.4 collective-permute-start
  86.5 4.3 collective-permute-done
  94.0 4.4 collective-permute-start
  98.4 4.1 collective-permute-done
  105.8 4.4 collective-permute-start
  110.2 4.1 collective-permute-done
  117.5 4.4 collective-permute-start
  121.9 4.1 collective-permute-done
  129.3 4.4 collective-permute-start
  133.7 4.1 collective-permute-done
  141.0 4.4 collective-permute-start
  145.4 4.4 collective-permute-done
  153.1 4.4 collective-permute-start
  157.5 4.1 collective-permute-done
  165.4 131.1 %while.40 = (s32[]{:T(128)}, bf16[16,8192]{1,0:T(8,128)(2,1)}, bf16[8,16,8192]{2,1,0:T(8,128)(2,1)}, bf16[8,16,64]{2,1,0:T(8,128)(2,1)}, pred[]{:T(512)}, /*inde...) while((s32[]{:T(128)}, bf16[16,8192]{1,0:T(8,128)(2,1)}, ...), condition=%wide.region_3.4_spmd, body=%wide.region_2.3_spmd.sunk | while | flops 34220040 | bytes 6834956 | solution.py:130
  167.0 1.9 bitcast_dynamic-update-slice_fusion.13
  171.4 7.3 %collective-permute-done.1 = bf16[16,8192]{1,0:T(8,128)(2,1)S(1)} collective-permute-done((bf16[16,8192]{1,0:T(8,128)(2,1)S(1)}, bf16[16,8192]{1,0:T(8,128)(2,1)S(1)}, u32[]{:S(2)}, u32[]{:S(2)}) %collective-permute-start.1) | collective-permute-done | bytes 262176 | tf_op jit(solution)/shard_map/while/body/eval_jaxpr/ppermute | solution.py:14
  185.5 8.4 %collective-permute-done.1 = bf16[16,8192]{1,0:T(8,128)(2,1)S(1)} collective-permute-done((bf16[16,8192]{1,0:T(8,128)(2,1)S(1)}, bf16[16,8192]{1,0:T(8,128)(2,1)S(1)}, u32[]{:S(2)}, u32[]{:S(2)}) %collective-permute-start.1) | collective-permute-done | bytes 262176 | tf_op jit(solution)/shard_map/while/body/eval_jaxpr/ppermute | solution.py:14
  200.6 9.6 %collective-permute-done.1 = bf16[16,8192]{1,0:T(8,128)(2,1)S(1)} collective-permute-done((bf16[16,8192]{1,0:T(8,128)(2,1)S(1)}, bf16[16,8192]{1,0:T(8,128)(2,1)S(1)}, u32[]{:S(2)}, u32[]{:S(2)}) %collective-permute-start.1) | collective-permute-done | bytes 262176 | tf_op jit(solution)/shard_map/while/body/eval_jaxpr/ppermute | solution.py:14
  216.9 8.9 %collective-permute-done.1 = bf16[16,8192]{1,0:T(8,128)(2,1)S(1)} collective-permute-done((bf16[16,8192]{1,0:T(8,128)(2,1)S(1)}, bf16[16,8192]{1,0:T(8,128)(2,1)S(1)}, u32[]{:S(2)}, u32[]{:S(2)}) %collective-permute-start.1) | collective-permute-done | bytes 262176 | tf_op jit(solution)/shard_map/while/body/eval_jaxpr/ppermute | solution.py:14
  232.6 8.1 %collective-permute-done.1 = bf16[16,8192]{1,0:T(8,128)(2,1)S(1)} collective-permute-done((bf16[16,8192]{1,0:T(8,128)(2,1)S(1)}, bf16[16,8192]{1,0:T(8,128)(2,1)S(1)}, u32[]{:S(2)}, u32[]{:S(2)}) %collective-permute-start.1) | collective-permute-done | bytes 262176 | tf_op jit(solution)/shard_map/while/body/eval_jaxpr/ppermute | solution.py:14
  247.4 7.2 %collective-permute-done.1 = bf16[16,8192]{1,0:T(8,128)(2,1)S(1)} collective-permute-done((bf16[16,8192]{1,0:T(8,128)(2,1)S(1)}, bf16[16,8192]{1,0:T(8,128)(2,1)S(1)}, u32[]{:S(2)}, u32[]{:S(2)}) %collective-permute-start.1) | collective-permute-done | bytes 262176 | tf_op jit(solution)/shard_map/while/body/eval_jaxpr/ppermute | solution.py:14
  261.3 7.0 %collective-permute-done.1 = bf16[16,8192]{1,0:T(8,128)(2,1)S(1)} collective-permute-done((bf16[16,8192]{1,0:T(8,128)(2,1)S(1)}, bf16[16,8192]{1,0:T(8,128)(2,1)S(1)}, u32[]{:S(2)}, u32[]{:S(2)}) %collective-permute-start.1) | collective-permute-done | bytes 262176 | tf_op jit(solution)/shard_map/while/body/eval_jaxpr/ppermute | solution.py:14
  275.0 7.0 %collective-permute-done.1 = bf16[16,8192]{1,0:T(8,128)(2,1)S(1)} collective-permute-done((bf16[16,8192]{1,0:T(8,128)(2,1)S(1)}, bf16[16,8192]{1,0:T(8,128)(2,1)S(1)}, u32[]{:S(2)}, u32[]{:S(2)}) %collective-permute-start.1) | collective-permute-done | bytes 262176 | tf_op jit(solution)/shard_map/while/body/eval_jaxpr/ppermute | solution.py:14
  288.7 7.0 %collective-permute-done.1 = bf16[16,8192]{1,0:T(8,128)(2,1)S(1)} collective-permute-done((bf16[16,8192]{1,0:T(8,128)(2,1)S(1)}, bf16[16,8192]{1,0:T(8,128)(2,1)S(1)}, u32[]{:S(2)}, u32[]{:S(2)}) %collective-permute-start.1) | collective-permute-done | bytes 262176 | tf_op jit(solution)/shard_map/while/body/eval_jaxpr/ppermute | solution.py:14
  296.4 2.2 convolution_bitcast_fusion.1
  299.8 3.0 reshape.406
  302.8 4.2 copy.14
  307.0 3.8 fusion.27
  310.8 3.5 fusion.14
  314.3 2.7 copy.11
  317.0 3.3 reshape.407
  320.3 23.0 %gather_fusion = f32[4096]{0:T(1024)S(1)} fusion(f32[524288]{0:T(1024)S(1)} %reshape.407, s32[4096]{0:T(1024)S(1)} %broadcast_clamp_fusion), kind=kCustom, calls=%fused_computation | custom fusion | bytes 49152 | tf_op jit(solution)/shard_map/gather | solution.py:146
  343.3 22.6 %scatter_custom_fusion = f32[524288]{0:T(1024)S(1)} fusion(s32[4096]{0:T(1024)S(1)} %bitcast.169, f32[4096]{0:T(1024)S(1)} %gather_fusion, f32[]{:T(128)} %constant.209.clone.1), kind=kCustom, calls=%fused_computation.46 | custom fusion | flops 4096 | bytes 2097156 | tf_op jit(solution)/shard_map/scatter-add | solution.py:147
  365.9 2.3 reshape.409
  368.2 3.5 copy.17
  371.7 2.2 fusion.25
  374.0 3.4 fusion.17
  377.4 2.7 copy.13
  380.1 5.0 %reshape.410 = f32[64,8192]{1,0:T(8,128)} reshape(f32[1,64,128,64]{3,2,1,0:T(8,128)} %copy.13) | data formatting | bytes 4194304 | tf_op jit(solution)/shard_map/reshape | solution.py:38
  385.1 2.7 fusion.20
  387.9 72.4 %all-reduce.1 = bf16[64,8192]{1,0:T(8,128)(2,1)} all-reduce(f32[64,8192]{1,0:T(8,128)} %reshape.410), channel_id=1, replica_groups=mesh['section'=2,'dp'=16] {'dp'}, use_global_device_ids=true, to_apply=%region_5.6 | all-reduce | flops 524288 | bytes 3145728 | tf_op jit(solution)/shard_map/psum | solution.py:150
  (199 shorter events, 96.2 us)
Async XLA Ops:
  7.2 2.6 copy-start.9
  7.2 38.2 %all-gather.3.cloned.1.call-start = ((), (), s32[]{:S(2)}) async-start(), calls=%async_computation | async-start | bytes 3145728 | tf_op jit(solution)/shard_map/all_gather | solution.py:67
  7.9 38.4 %copy-start = (bf16[1,64,8192]{2,1,0:T(8,128)(2,1)S(1)}, bf16[1,64,8192]{2,1,0:T(8,128)(2,1)}, u32[]{:S(2)}) copy-start(bf16[1,64,8192]{2,1,0:T(8,128)(2,1)} %param.11) | copy-start | bytes 3145732
  7.9 154.4 %all-gather.5.cloned.1.call-start = ((), (), s32[]{:S(2)}) async-start(), calls=%async_computation.1 | async-start | bytes 3145728 | tf_op jit(solution)/shard_map/all_gather | solution.py:68
  48.9 11.1 %collective-permute-start = (bf16[16,8192]{1,0:T(8,128)(2,1)}, bf16[16,8192]{1,0:T(8,128)(2,1)S(1)}, u32[]{:S(2)}, u32[]{:S(2)}) collective-permute-start(bf16[16,8192]{1,0:T(8,128)(2,1)} %fusion.98), channel_id=1, source_target_pairs={{0,16},{1,17},{2,18},{3,19},{4,20},{5,21},{6,22},{7,23},{8,24},{9,... | collective-permute-start | bytes 786440 | tf_op jit(solution)/shard_map/while/body/eval_jaxpr/ppermute | solution.py:14
  60.0 0.7 copy-start.5
  63.2 15.6 %collective-permute-start = (bf16[16,8192]{1,0:T(8,128)(2,1)}, bf16[16,8192]{1,0:T(8,128)(2,1)S(1)}, u32[]{:S(2)}, u32[]{:S(2)}) collective-permute-start(bf16[16,8192]{1,0:T(8,128)(2,1)} %fusion.98), channel_id=1, source_target_pairs={{0,16},{1,17},{2,18},{3,19},{4,20},{5,21},{6,22},{7,23},{8,24},{9,... | collective-permute-start | bytes 786440 | tf_op jit(solution)/shard_map/while/body/eval_jaxpr/ppermute | solution.py:14
  78.8 0.7 copy-start.5
  82.1 8.7 %collective-permute-start = (bf16[16,8192]{1,0:T(8,128)(2,1)}, bf16[16,8192]{1,0:T(8,128)(2,1)S(1)}, u32[]{:S(2)}, u32[]{:S(2)}) collective-permute-start(bf16[16,8192]{1,0:T(8,128)(2,1)} %fusion.98), channel_id=1, source_target_pairs={{0,16},{1,17},{2,18},{3,19},{4,20},{5,21},{6,22},{7,23},{8,24},{9,... | collective-permute-start | bytes 786440 | tf_op jit(solution)/shard_map/while/body/eval_jaxpr/ppermute | solution.py:14
  90.8 0.7 copy-start.5
  94.0 8.5 %collective-permute-start = (bf16[16,8192]{1,0:T(8,128)(2,1)}, bf16[16,8192]{1,0:T(8,128)(2,1)S(1)}, u32[]{:S(2)}, u32[]{:S(2)}) collective-permute-start(bf16[16,8192]{1,0:T(8,128)(2,1)} %fusion.98), channel_id=1, source_target_pairs={{0,16},{1,17},{2,18},{3,19},{4,20},{5,21},{6,22},{7,23},{8,24},{9,... | collective-permute-start | bytes 786440 | tf_op jit(solution)/shard_map/while/body/eval_jaxpr/ppermute | solution.py:14
  102.6 0.7 copy-start.5
  105.8 8.5 %collective-permute-start = (bf16[16,8192]{1,0:T(8,128)(2,1)}, bf16[16,8192]{1,0:T(8,128)(2,1)S(1)}, u32[]{:S(2)}, u32[]{:S(2)}) collective-permute-start(bf16[16,8192]{1,0:T(8,128)(2,1)} %fusion.98), channel_id=1, source_target_pairs={{0,16},{1,17},{2,18},{3,19},{4,20},{5,21},{6,22},{7,23},{8,24},{9,... | collective-permute-start | bytes 786440 | tf_op jit(solution)/shard_map/while/body/eval_jaxpr/ppermute | solution.py:14
  114.3 0.7 copy-start.5
  117.5 8.5 %collective-permute-start = (bf16[16,8192]{1,0:T(8,128)(2,1)}, bf16[16,8192]{1,0:T(8,128)(2,1)S(1)}, u32[]{:S(2)}, u32[]{:S(2)}) collective-permute-start(bf16[16,8192]{1,0:T(8,128)(2,1)} %fusion.98), channel_id=1, source_target_pairs={{0,16},{1,17},{2,18},{3,19},{4,20},{5,21},{6,22},{7,23},{8,24},{9,... | collective-permute-start | bytes 786440 | tf_op jit(solution)/shard_map/while/body/eval_jaxpr/ppermute | solution.py:14
  126.1 0.7 copy-start.5
  129.3 8.5 %collective-permute-start = (bf16[16,8192]{1,0:T(8,128)(2,1)}, bf16[16,8192]{1,0:T(8,128)(2,1)S(1)}, u32[]{:S(2)}, u32[]{:S(2)}) collective-permute-start(bf16[16,8192]{1,0:T(8,128)(2,1)} %fusion.98), channel_id=1, source_target_pairs={{0,16},{1,17},{2,18},{3,19},{4,20},{5,21},{6,22},{7,23},{8,24},{9,... | collective-permute-start | bytes 786440 | tf_op jit(solution)/shard_map/while/body/eval_jaxpr/ppermute | solution.py:14
  137.8 0.7 copy-start.5
  141.0 8.8 %collective-permute-start = (bf16[16,8192]{1,0:T(8,128)(2,1)}, bf16[16,8192]{1,0:T(8,128)(2,1)S(1)}, u32[]{:S(2)}, u32[]{:S(2)}) collective-permute-start(bf16[16,8192]{1,0:T(8,128)(2,1)} %fusion.98), channel_id=1, source_target_pairs={{0,16},{1,17},{2,18},{3,19},{4,20},{5,21},{6,22},{7,23},{8,24},{9,... | collective-permute-start | bytes 786440 | tf_op jit(solution)/shard_map/while/body/eval_jaxpr/ppermute | solution.py:14
  149.8 0.7 copy-start.5
  153.1 8.5 %collective-permute-start = (bf16[16,8192]{1,0:T(8,128)(2,1)}, bf16[16,8192]{1,0:T(8,128)(2,1)S(1)}, u32[]{:S(2)}, u32[]{:S(2)}) collective-permute-start(bf16[16,8192]{1,0:T(8,128)(2,1)} %fusion.98), channel_id=1, source_target_pairs={{0,16},{1,17},{2,18},{3,19},{4,20},{5,21},{6,22},{7,23},{8,24},{9,... | collective-permute-start | bytes 786440 | tf_op jit(solution)/shard_map/while/body/eval_jaxpr/ppermute | solution.py:14
  161.6 0.7 copy-start.5
  162.3 3.1 copy-start.3
  170.1 8.6 %collective-permute-start.1 = (bf16[16,8192]{1,0:T(8,128)(2,1)S(1)}, bf16[16,8192]{1,0:T(8,128)(2,1)S(1)}, u32[]{:S(2)}, u32[]{:S(2)}) collective-permute-start(bf16[16,8192]{1,0:T(8,128)(2,1)S(1)} %fusion.103), channel_id=1, source_target_pairs={{16,0},{17,1},{18,2},{19,3},{20,4},{21,5},{22,6},{23,7},{24,8},{25... | collective-permute-start | bytes 786440 | tf_op jit(solution)/shard_map/while/body/eval_jaxpr/ppermute | solution.py:14
  178.7 0.7 copy-start.6
  184.1 9.7 %collective-permute-start.1 = (bf16[16,8192]{1,0:T(8,128)(2,1)S(1)}, bf16[16,8192]{1,0:T(8,128)(2,1)S(1)}, u32[]{:S(2)}, u32[]{:S(2)}) collective-permute-start(bf16[16,8192]{1,0:T(8,128)(2,1)S(1)} %fusion.103), channel_id=1, source_target_pairs={{16,0},{17,1},{18,2},{19,3},{20,4},{21,5},{22,6},{23,7},{24,8},{25... | collective-permute-start | bytes 786440 | tf_op jit(solution)/shard_map/while/body/eval_jaxpr/ppermute | solution.py:14
  193.9 0.7 copy-start.6
  199.3 10.9 %collective-permute-start.1 = (bf16[16,8192]{1,0:T(8,128)(2,1)S(1)}, bf16[16,8192]{1,0:T(8,128)(2,1)S(1)}, u32[]{:S(2)}, u32[]{:S(2)}) collective-permute-start(bf16[16,8192]{1,0:T(8,128)(2,1)S(1)} %fusion.103), channel_id=1, source_target_pairs={{16,0},{17,1},{18,2},{19,3},{20,4},{21,5},{22,6},{23,7},{24,8},{25... | collective-permute-start | bytes 786440 | tf_op jit(solution)/shard_map/while/body/eval_jaxpr/ppermute | solution.py:14
  210.2 0.7 copy-start.6
  215.6 10.2 %collective-permute-start.1 = (bf16[16,8192]{1,0:T(8,128)(2,1)S(1)}, bf16[16,8192]{1,0:T(8,128)(2,1)S(1)}, u32[]{:S(2)}, u32[]{:S(2)}) collective-permute-start(bf16[16,8192]{1,0:T(8,128)(2,1)S(1)} %fusion.103), channel_id=1, source_target_pairs={{16,0},{17,1},{18,2},{19,3},{20,4},{21,5},{22,6},{23,7},{24,8},{25... | collective-permute-start | bytes 786440 | tf_op jit(solution)/shard_map/while/body/eval_jaxpr/ppermute | solution.py:14
  225.8 0.7 copy-start.6
  231.3 9.4 %collective-permute-start.1 = (bf16[16,8192]{1,0:T(8,128)(2,1)S(1)}, bf16[16,8192]{1,0:T(8,128)(2,1)S(1)}, u32[]{:S(2)}, u32[]{:S(2)}) collective-permute-start(bf16[16,8192]{1,0:T(8,128)(2,1)S(1)} %fusion.103), channel_id=1, source_target_pairs={{16,0},{17,1},{18,2},{19,3},{20,4},{21,5},{22,6},{23,7},{24,8},{25... | collective-permute-start | bytes 786440 | tf_op jit(solution)/shard_map/while/body/eval_jaxpr/ppermute | solution.py:14
  240.6 0.7 copy-start.6
  246.1 8.5 %collective-permute-start.1 = (bf16[16,8192]{1,0:T(8,128)(2,1)S(1)}, bf16[16,8192]{1,0:T(8,128)(2,1)S(1)}, u32[]{:S(2)}, u32[]{:S(2)}) collective-permute-start(bf16[16,8192]{1,0:T(8,128)(2,1)S(1)} %fusion.103), channel_id=1, source_target_pairs={{16,0},{17,1},{18,2},{19,3},{20,4},{21,5},{22,6},{23,7},{24,8},{25... | collective-permute-start | bytes 786440 | tf_op jit(solution)/shard_map/while/body/eval_jaxpr/ppermute | solution.py:14
  254.6 0.7 copy-start.6
  260.0 8.3 %collective-permute-start.1 = (bf16[16,8192]{1,0:T(8,128)(2,1)S(1)}, bf16[16,8192]{1,0:T(8,128)(2,1)S(1)}, u32[]{:S(2)}, u32[]{:S(2)}) collective-permute-start(bf16[16,8192]{1,0:T(8,128)(2,1)S(1)} %fusion.103), channel_id=1, source_target_pairs={{16,0},{17,1},{18,2},{19,3},{20,4},{21,5},{22,6},{23,7},{24,8},{25... | collective-permute-start | bytes 786440 | tf_op jit(solution)/shard_map/while/body/eval_jaxpr/ppermute | solution.py:14
  268.3 0.7 copy-start.6
  273.7 8.3 %collective-permute-start.1 = (bf16[16,8192]{1,0:T(8,128)(2,1)S(1)}, bf16[16,8192]{1,0:T(8,128)(2,1)S(1)}, u32[]{:S(2)}, u32[]{:S(2)}) collective-permute-start(bf16[16,8192]{1,0:T(8,128)(2,1)S(1)} %fusion.103), channel_id=1, source_target_pairs={{16,0},{17,1},{18,2},{19,3},{20,4},{21,5},{22,6},{23,7},{24,8},{25... | collective-permute-start | bytes 786440 | tf_op jit(solution)/shard_map/while/body/eval_jaxpr/ppermute | solution.py:14
  282.0 0.7 copy-start.6
  287.4 8.3 %collective-permute-start.1 = (bf16[16,8192]{1,0:T(8,128)(2,1)S(1)}, bf16[16,8192]{1,0:T(8,128)(2,1)S(1)}, u32[]{:S(2)}, u32[]{:S(2)}) collective-permute-start(bf16[16,8192]{1,0:T(8,128)(2,1)S(1)} %fusion.103), channel_id=1, source_target_pairs={{16,0},{17,1},{18,2},{19,3},{20,4},{21,5},{22,6},{23,7},{24,8},{25... | collective-permute-start | bytes 786440 | tf_op jit(solution)/shard_map/while/body/eval_jaxpr/ppermute | solution.py:14
  295.7 0.7 copy-start.6
  296.4 2.2 copy-start.4
  296.4 2.5 copy-start.7
  296.4 2.5 copy-start.8
  299.8 3.0 copy-start.1
  302.8 4.2 copy-start.10
  302.8 4.2 copy-start.11
  380.1 5.0 %copy-start.2 = (f32[64,8192]{1,0:T(8,128)S(1)}, f32[64,8192]{1,0:T(8,128)}, u32[]{:S(2)}) copy-start(f32[64,8192]{1,0:T(8,128)} %copy-done.1) | copy-start | bytes 6291460
Sparse Core Ops, SparseCore 0:
  9.5 35.8 all-gather.2
  46.9 39.2 all-gather.4
where the time goes:
time: 469 us; the launch traced here: 467 us
  waiting for transfers between devices  156 us (33%)
  local copies, waits for them, and re-layouts  82.7 us (18%)
  blocking collectives  72.4 us (15%)
  other arithmetic  52.9 us (11%)
  starting transfers between devices  48.9 us (10%)
  matrix products  39.7 us (8%)
  between operations  14.2 us (3%)
    ppermute x18, waiting for transfers between devices, from_behind(): lax.ppermute(value, axis, [(source, source + steps) for source in range(l...  120 us
    psum x1, blocking collectives, local(): update = lax.psum(own_field, 'dp')  72.4 us
    ppermute x18, starting transfers between devices, from_behind(): lax.ppermute(value, axis, [(source, source + steps) for source in range(l...  48.8 us
    all_gather x1, waiting for transfers between devices, local(): lax.all_gather(inputs, 'section', axis=1, tiled=True)  34.7 us
    dynamic_update_slice x27, other arithmetic, store_slot(): lax.dynamic_update_index_in_dim(saved, jnp.where(is_valid, value, previou...  26.2 us
    gather x1, local copies, waits for them, and re-layouts, local(): kept_values = coeffs[offsets]  23 us
    scatter-add x1, other arithmetic, local(): jnp.zeros_like(coeffs).at[offsets.reshape(-1)].add(kept_values.reshape(-1))  22.6 us
    dynamic_slice x45, local copies, waits for them, and re-layouts, store_slot(): previous = lax.dynamic_index_in_dim(saved, slot_clip, 0, keepdims=False)  15.3 us
  transfers between devices with their start and end apart: 20, of which 19 were waited for; matrix products, arithmetic and copies ran while one was open for 5% of the time, Pallas kernels for 0%

commit v1 on v0

--- a/solution.py
+++ b/solution.py
@@ -147,7 +147,7 @@
     own_sparse = jnp.zeros_like(coeffs).at[offsets.reshape(-1)].add(kept_values.reshape(-1))
     own_field = inverse_groups(own_sparse, dct_table, row_count, columns)
     momentum_out = (momentum_new - own_field).astype(jnp.bfloat16)
-    update = lax.psum(own_field, "dp")
+    update = jnp.sum(lax.all_gather(own_field, "dp"), axis=0)
     return (momentum_out[None, None], update.astype(jnp.bfloat16)[None, None])
 
 

time: 469 us -> 601 us (1.28)
  waiting for transfers between devices: 156 us -> 342 us
  blocking collectives: 72.4 us -> 0 us
  other arithmetic: 52.9 us -> 65.7 us
    all_gather x0 -> x1, waiting for transfers between devices: none -> 160 us  [local(): update = jnp.sum(lax.all_gather(own_field, 'dp'), axis=0)]
    psum x1 -> x0, blocking collectives: 72.4 us -> none  [local(): update = lax.psum(own_field, 'dp')]
    all_gather x1, waiting for transfers between devices: 0.01 us -> 34.7 us  [local(): lax.all_gather(cotangent, 'section', axis=1, tiled=True)]
    reduce_sum x0 -> x1, other arithmetic: none -> 12.8 us  [local(): update = jnp.sum(lax.all_gather(own_field, 'dp'), axis=0)]
    ppermute x18, waiting for transfers between devices: 120 us -> 111 us  [from_behind(): lax.ppermute(value, axis, [(source, source + steps) for source in range(l...]
    another operation x8 -> x9, local copies, waits for them, and re-layouts: 9.8 us -> 14.5 us
  transfers between devices with their start and end apart: 20 -> 21, of which waited for: 19 -> 21; matrix products, arithmetic and copies ran while one was open for 5% -> 2% of each run, Pallas kernels for 0% -> 0%
where the time goes in v1:
time: 601 us; the launch traced here: 599 us
  waiting for transfers between devices  342 us (57%)
  local copies, waits for them, and re-layouts  87.3 us (15%)
  other arithmetic  65.7 us (11%)
  starting transfers between devices  49 us (8%)
  matrix products  40.4 us (7%)
  between operations  13.9 us (2%)
    all_gather x1, waiting for transfers between devices, local(): update = jnp.sum(lax.all_gather(own_field, 'dp'), axis=0)  160 us
    ppermute x18, waiting for transfers between devices, from_behind(): lax.ppermute(value, axis, [(source, source + steps) for source in range(l...  111 us
    ppermute x18, starting transfers between devices, from_behind(): lax.ppermute(value, axis, [(source, source + steps) for source in range(l...  48.8 us
    all_gather x1, waiting for transfers between devices, local(): lax.all_gather(cotangent, 'section', axis=1, tiled=True)  34.7 us
    all_gather x1, waiting for transfers between devices, local(): lax.all_gather(inputs, 'section', axis=1, tiled=True)  34.6 us
    dynamic_update_slice x27, other arithmetic, store_slot(): lax.dynamic_update_index_in_dim(saved, jnp.where(is_valid, value, previou...  26.3 us
    gather x1, local copies, waits for them, and re-layouts, local(): kept_values = coeffs[offsets]  23 us
    scatter-add x1, other arithmetic, local(): jnp.zeros_like(coeffs).at[offsets.reshape(-1)].add(kept_values.reshape(-1))  22.6 us
  transfers between devices with their start and end apart: 21, of which 21 were waited for; matrix products, arithmetic and copies ran while one was open for 2% of the time, Pallas kernels for 0%

profile of v1, /device:TPU:0, one launch (start us, length us, event | category | flops | bytes accessed | tf_op | source)
XLA Modules:
  0.0 598.9 jit_solution(10184977070354423985)
XLA Ops:
  10.8 34.6 %all-gather.4.cloned.1.call-done = bf16[128,8192]{1,0:T(8,128)(2,1)} async-done(((bf16[128,4096]{1,0:T(8,128)(2,1)}), bf16[128,8192]{1,0:T(8,128)(2,1)}) %all-gather.4.cloned.1.call-update) | async-done | bytes 2097168 | tf_op jit(solution)/shard_map/all_gather | solution.py:67
  45.4 34.7 %all-gather.6.cloned.1.call-done = bf16[128,8192]{1,0:T(8,128)(2,1)} async-done(((bf16[128,4096]{1,0:T(8,128)(2,1)}), bf16[128,8192]{1,0:T(8,128)(2,1)}) %all-gather.6.cloned.1.call-update) | async-done | bytes 2097168 | tf_op jit(solution)/shard_map/all_gather | solution.py:68
  81.0 107.0 %while.39 = (s32[]{:T(128)}, bf16[16,8192]{1,0:T(8,128)(2,1)}, bf16[8,16,8192]{2,1,0:T(8,128)(2,1)S(1)}, bf16[8,16,64]{2,1,0:T(8,128)(2,1)S(1)}, f32[8,16,64]{2,...) while((s32[]{:T(128)}, bf16[16,8192]{1,0:T(8,128)(2,1)}, ...), condition=%wide.region_1.2_spmd, body=%wide.region_0.1_spmd.sunk | while | flops 34222088 | bytes 6873366 | solution.py:103
  83.5 2.3 collective-permute-start
  85.9 5.8 collective-permute-done
  95.0 4.4 collective-permute-start
  99.4 5.0 collective-permute-done
  107.5 4.4 collective-permute-start
  111.9 4.1 collective-permute-done
  119.3 4.4 collective-permute-start
  123.7 4.1 collective-permute-done
  131.0 4.4 collective-permute-start
  135.4 4.1 collective-permute-done
  142.8 4.4 collective-permute-start
  147.2 4.1 collective-permute-done
  154.5 4.4 collective-permute-start
  158.9 4.1 collective-permute-done
  166.2 4.4 collective-permute-start
  170.6 4.9 collective-permute-done
  178.8 4.4 collective-permute-start
  183.2 4.1 collective-permute-done
  191.0 131.2 %while.40 = (s32[]{:T(128)}, bf16[16,8192]{1,0:T(8,128)(2,1)}, bf16[8,16,8192]{2,1,0:T(8,128)(2,1)}, bf16[8,16,64]{2,1,0:T(8,128)(2,1)}, pred[]{:T(512)}, /*inde...) while((s32[]{:T(128)}, bf16[16,8192]{1,0:T(8,128)(2,1)}, ...), condition=%wide.region_3.4_spmd, body=%wide.region_2.3_spmd.sunk | while | flops 34220040 | bytes 6834956 | solution.py:130
  197.0 7.7 %collective-permute-done.1 = bf16[16,8192]{1,0:T(8,128)(2,1)S(1)} collective-permute-done((bf16[16,8192]{1,0:T(8,128)(2,1)S(1)}, bf16[16,8192]{1,0:T(8,128)(2,1)S(1)}, u32[]{:S(2)}, u32[]{:S(2)}) %collective-permute-start.1) | collective-permute-done | bytes 262176 | tf_op jit(solution)/shard_map/while/body/eval_jaxpr/ppermute | solution.py:14
  211.5 8.9 %collective-permute-done.1 = bf16[16,8192]{1,0:T(8,128)(2,1)S(1)} collective-permute-done((bf16[16,8192]{1,0:T(8,128)(2,1)S(1)}, bf16[16,8192]{1,0:T(8,128)(2,1)S(1)}, u32[]{:S(2)}, u32[]{:S(2)}) %collective-permute-start.1) | collective-permute-done | bytes 262176 | tf_op jit(solution)/shard_map/while/body/eval_jaxpr/ppermute | solution.py:14
  227.2 9.5 %collective-permute-done.1 = bf16[16,8192]{1,0:T(8,128)(2,1)S(1)} collective-permute-done((bf16[16,8192]{1,0:T(8,128)(2,1)S(1)}, bf16[16,8192]{1,0:T(8,128)(2,1)S(1)}, u32[]{:S(2)}, u32[]{:S(2)}) %collective-permute-start.1) | collective-permute-done | bytes 262176 | tf_op jit(solution)/shard_map/while/body/eval_jaxpr/ppermute | solution.py:14
  243.5 8.6 %collective-permute-done.1 = bf16[16,8192]{1,0:T(8,128)(2,1)S(1)} collective-permute-done((bf16[16,8192]{1,0:T(8,128)(2,1)S(1)}, bf16[16,8192]{1,0:T(8,128)(2,1)S(1)}, u32[]{:S(2)}, u32[]{:S(2)}) %collective-permute-start.1) | collective-permute-done | bytes 262176 | tf_op jit(solution)/shard_map/while/body/eval_jaxpr/ppermute | solution.py:14
  258.9 7.8 %collective-permute-done.1 = bf16[16,8192]{1,0:T(8,128)(2,1)S(1)} collective-permute-done((bf16[16,8192]{1,0:T(8,128)(2,1)S(1)}, bf16[16,8192]{1,0:T(8,128)(2,1)S(1)}, u32[]{:S(2)}, u32[]{:S(2)}) %collective-permute-start.1) | collective-permute-done | bytes 262176 | tf_op jit(solution)/shard_map/while/body/eval_jaxpr/ppermute | solution.py:14
  273.4 7.0 %collective-permute-done.1 = bf16[16,8192]{1,0:T(8,128)(2,1)S(1)} collective-permute-done((bf16[16,8192]{1,0:T(8,128)(2,1)S(1)}, bf16[16,8192]{1,0:T(8,128)(2,1)S(1)}, u32[]{:S(2)}, u32[]{:S(2)}) %collective-permute-start.1) | collective-permute-done | bytes 262176 | tf_op jit(solution)/shard_map/while/body/eval_jaxpr/ppermute | solution.py:14
  287.1 7.0 %collective-permute-done.1 = bf16[16,8192]{1,0:T(8,128)(2,1)S(1)} collective-permute-done((bf16[16,8192]{1,0:T(8,128)(2,1)S(1)}, bf16[16,8192]{1,0:T(8,128)(2,1)S(1)}, u32[]{:S(2)}, u32[]{:S(2)}) %collective-permute-start.1) | collective-permute-done | bytes 262176 | tf_op jit(solution)/shard_map/while/body/eval_jaxpr/ppermute | solution.py:14
  300.8 7.0 %collective-permute-done.1 = bf16[16,8192]{1,0:T(8,128)(2,1)S(1)} collective-permute-done((bf16[16,8192]{1,0:T(8,128)(2,1)S(1)}, bf16[16,8192]{1,0:T(8,128)(2,1)S(1)}, u32[]{:S(2)}, u32[]{:S(2)}) %collective-permute-start.1) | collective-permute-done | bytes 262176 | tf_op jit(solution)/shard_map/while/body/eval_jaxpr/ppermute | solution.py:14
  314.5 7.0 %collective-permute-done.1 = bf16[16,8192]{1,0:T(8,128)(2,1)S(1)} collective-permute-done((bf16[16,8192]{1,0:T(8,128)(2,1)S(1)}, bf16[16,8192]{1,0:T(8,128)(2,1)S(1)}, u32[]{:S(2)}, u32[]{:S(2)}) %collective-permute-start.1) | collective-permute-done | bytes 262176 | tf_op jit(solution)/shard_map/while/body/eval_jaxpr/ppermute | solution.py:14
  326.3 3.0 reshape.414
  329.3 4.2 copy.16
  333.5 3.8 fusion.27
  337.3 3.5 fusion.14
  340.8 2.7 copy.20
  343.5 3.3 reshape.415
  346.7 23.0 %gather_fusion = f32[4096]{0:T(1024)S(1)} fusion(f32[524288]{0:T(1024)S(1)} %reshape.415, s32[4096]{0:T(1024)S(1)} %broadcast_clamp_fusion), kind=kCustom, calls=%fused_computation | custom fusion | bytes 49152 | tf_op jit(solution)/shard_map/gather | solution.py:146
  369.8 22.6 %scatter_custom_fusion = f32[524288]{0:T(1024)S(1)} fusion(s32[4096]{0:T(1024)S(1)} %bitcast.172, f32[4096]{0:T(1024)S(1)} %gather_fusion, f32[]{:T(128)} %constant.210.clone.1), kind=kCustom, calls=%fused_computation.46 | custom fusion | flops 4096 | bytes 2097156 | tf_op jit(solution)/shard_map/scatter-add | solution.py:147
  392.4 2.3 reshape.417
  394.7 3.5 copy.22
  400.5 3.4 fusion.17
  403.9 2.8 copy.24
  406.7 4.8 all_gather_reshape.3
  411.6 4.9 reshape.418
  416.5 2.7 fusion.20
  419.2 160.4 %all-gather.8.cloned.1.call-done = f32[16,64,8192]{2,1,0:T(8,128)} async-done(((f32[1,64,8192]{2,1,0:T(8,128)}), f32[16,64,8192]{2,1,0:T(8,128)}) %all-gather.8.cloned.1.call-update) | async-done | bytes 33554448 | tf_op jit(solution)/shard_map/all_gather | solution.py:150
  579.6 12.8 %reduce_sum.9 = bf16[64,8192]{1,0:T(8,128)(2,1)} reduce(f32[16,64,8192]{2,1,0:T(8,128)} %all-gather.8.cloned.1.call-done, f32[]{:T(128)} %constant.210.clone.1), dimensions={0}, to_apply=%region_5.6 | reduce | flops 7864320 | bytes 34603012 | tf_op jit(solution)/shard_map/reduce_sum | solution.py:150
  (201 shorter events, 103.2 us)
Async XLA Ops:
  7.2 1.6 copy-start.8
  7.2 38.2 %all-gather.4.cloned.1.call-start = ((), (), s32[]{:S(2)}) async-start(), calls=%async_computation | async-start | bytes 3145728 | tf_op jit(solution)/shard_map/all_gather | solution.py:67
  7.9 73.1 %copy-start = (bf16[1,64,8192]{2,1,0:T(8,128)(2,1)S(1)}, bf16[1,64,8192]{2,1,0:T(8,128)(2,1)}, u32[]{:S(2)}) copy-start(bf16[1,64,8192]{2,1,0:T(8,128)(2,1)} %param.11) | copy-start | bytes 3145732
  7.9 72.1 %all-gather.6.cloned.1.call-start = ((), (), s32[]{:S(2)}) async-start(), calls=%async_computation.1 | async-start | bytes 3145728 | tf_op jit(solution)/shard_map/all_gather | solution.py:68
  8.7 570.9 %all-gather.8.cloned.1.call-start = ((), (), s32[]{:S(2)}) async-start(), calls=%async_computation.2 | async-start | bytes 35651584 | tf_op jit(solution)/shard_map/all_gather | solution.py:150
  83.5 8.2 %collective-permute-start = (bf16[16,8192]{1,0:T(8,128)(2,1)}, bf16[16,8192]{1,0:T(8,128)(2,1)S(1)}, u32[]{:S(2)}, u32[]{:S(2)}) collective-permute-start(bf16[16,8192]{1,0:T(8,128)(2,1)} %fusion.98), channel_id=1, source_target_pairs={{0,16},{1,17},{2,18},{3,19},{4,20},{5,21},{6,22},{7,23},{8,24},{9,... | collective-permute-start | bytes 786440 | tf_op jit(solution)/shard_map/while/body/eval_jaxpr/ppermute | solution.py:14
  91.8 0.7 copy-start.5
  95.0 9.4 %collective-permute-start = (bf16[16,8192]{1,0:T(8,128)(2,1)}, bf16[16,8192]{1,0:T(8,128)(2,1)S(1)}, u32[]{:S(2)}, u32[]{:S(2)}) collective-permute-start(bf16[16,8192]{1,0:T(8,128)(2,1)} %fusion.98), channel_id=1, source_target_pairs={{0,16},{1,17},{2,18},{3,19},{4,20},{5,21},{6,22},{7,23},{8,24},{9,... | collective-permute-start | bytes 786440 | tf_op jit(solution)/shard_map/while/body/eval_jaxpr/ppermute | solution.py:14
  104.3 0.7 copy-start.5
  107.5 8.5 %collective-permute-start = (bf16[16,8192]{1,0:T(8,128)(2,1)}, bf16[16,8192]{1,0:T(8,128)(2,1)S(1)}, u32[]{:S(2)}, u32[]{:S(2)}) collective-permute-start(bf16[16,8192]{1,0:T(8,128)(2,1)} %fusion.98), channel_id=1, source_target_pairs={{0,16},{1,17},{2,18},{3,19},{4,20},{5,21},{6,22},{7,23},{8,24},{9,... | collective-permute-start | bytes 786440 | tf_op jit(solution)/shard_map/while/body/eval_jaxpr/ppermute | solution.py:14
  116.1 0.7 copy-start.5
  119.3 8.5 %collective-permute-start = (bf16[16,8192]{1,0:T(8,128)(2,1)}, bf16[16,8192]{1,0:T(8,128)(2,1)S(1)}, u32[]{:S(2)}, u32[]{:S(2)}) collective-permute-start(bf16[16,8192]{1,0:T(8,128)(2,1)} %fusion.98), channel_id=1, source_target_pairs={{0,16},{1,17},{2,18},{3,19},{4,20},{5,21},{6,22},{7,23},{8,24},{9,... | collective-permute-start | bytes 786440 | tf_op jit(solution)/shard_map/while/body/eval_jaxpr/ppermute | solution.py:14
  127.8 0.7 copy-start.5
  131.0 8.5 %collective-permute-start = (bf16[16,8192]{1,0:T(8,128)(2,1)}, bf16[16,8192]{1,0:T(8,128)(2,1)S(1)}, u32[]{:S(2)}, u32[]{:S(2)}) collective-permute-start(bf16[16,8192]{1,0:T(8,128)(2,1)} %fusion.98), channel_id=1, source_target_pairs={{0,16},{1,17},{2,18},{3,19},{4,20},{5,21},{6,22},{7,23},{8,24},{9,... | collective-permute-start | bytes 786440 | tf_op jit(solution)/shard_map/while/body/eval_jaxpr/ppermute | solution.py:14
  139.6 0.7 copy-start.5
  142.8 8.5 %collective-permute-start = (bf16[16,8192]{1,0:T(8,128)(2,1)}, bf16[16,8192]{1,0:T(8,128)(2,1)S(1)}, u32[]{:S(2)}, u32[]{:S(2)}) collective-permute-start(bf16[16,8192]{1,0:T(8,128)(2,1)} %fusion.98), channel_id=1, source_target_pairs={{0,16},{1,17},{2,18},{3,19},{4,20},{5,21},{6,22},{7,23},{8,24},{9,... | collective-permute-start | bytes 786440 | tf_op jit(solution)/shard_map/while/body/eval_jaxpr/ppermute | solution.py:14
  151.3 0.7 copy-start.5
  154.5 8.5 %collective-permute-start = (bf16[16,8192]{1,0:T(8,128)(2,1)}, bf16[16,8192]{1,0:T(8,128)(2,1)S(1)}, u32[]{:S(2)}, u32[]{:S(2)}) collective-permute-start(bf16[16,8192]{1,0:T(8,128)(2,1)} %fusion.98), channel_id=1, source_target_pairs={{0,16},{1,17},{2,18},{3,19},{4,20},{5,21},{6,22},{7,23},{8,24},{9,... | collective-permute-start | bytes 786440 | tf_op jit(solution)/shard_map/while/body/eval_jaxpr/ppermute | solution.py:14
  163.0 0.7 copy-start.5
  166.2 9.3 %collective-permute-start = (bf16[16,8192]{1,0:T(8,128)(2,1)}, bf16[16,8192]{1,0:T(8,128)(2,1)S(1)}, u32[]{:S(2)}, u32[]{:S(2)}) collective-permute-start(bf16[16,8192]{1,0:T(8,128)(2,1)} %fusion.98), channel_id=1, source_target_pairs={{0,16},{1,17},{2,18},{3,19},{4,20},{5,21},{6,22},{7,23},{8,24},{9,... | collective-permute-start | bytes 786440 | tf_op jit(solution)/shard_map/while/body/eval_jaxpr/ppermute | solution.py:14
  175.6 0.7 copy-start.5
  178.8 8.5 %collective-permute-start = (bf16[16,8192]{1,0:T(8,128)(2,1)}, bf16[16,8192]{1,0:T(8,128)(2,1)S(1)}, u32[]{:S(2)}, u32[]{:S(2)}) collective-permute-start(bf16[16,8192]{1,0:T(8,128)(2,1)} %fusion.98), channel_id=1, source_target_pairs={{0,16},{1,17},{2,18},{3,19},{4,20},{5,21},{6,22},{7,23},{8,24},{9,... | collective-permute-start | bytes 786440 | tf_op jit(solution)/shard_map/while/body/eval_jaxpr/ppermute | solution.py:14
  187.3 0.7 copy-start.5
  188.0 2.9 copy-start.3
  195.7 9.1 %collective-permute-start.1 = (bf16[16,8192]{1,0:T(8,128)(2,1)S(1)}, bf16[16,8192]{1,0:T(8,128)(2,1)S(1)}, u32[]{:S(2)}, u32[]{:S(2)}) collective-permute-start(bf16[16,8192]{1,0:T(8,128)(2,1)S(1)} %fusion.103), channel_id=1, source_target_pairs={{16,0},{17,1},{18,2},{19,3},{20,4},{21,5},{22,6},{23,7},{24,8},{25... | collective-permute-start | bytes 786440 | tf_op jit(solution)/shard_map/while/body/eval_jaxpr/ppermute | solution.py:14
  204.8 0.7 copy-start.6
  210.2 10.2 %collective-permute-start.1 = (bf16[16,8192]{1,0:T(8,128)(2,1)S(1)}, bf16[16,8192]{1,0:T(8,128)(2,1)S(1)}, u32[]{:S(2)}, u32[]{:S(2)}) collective-permute-start(bf16[16,8192]{1,0:T(8,128)(2,1)S(1)} %fusion.103), channel_id=1, source_target_pairs={{16,0},{17,1},{18,2},{19,3},{20,4},{21,5},{22,6},{23,7},{24,8},{25... | collective-permute-start | bytes 786440 | tf_op jit(solution)/shard_map/while/body/eval_jaxpr/ppermute | solution.py:14
  220.4 0.7 copy-start.6
  225.9 10.8 %collective-permute-start.1 = (bf16[16,8192]{1,0:T(8,128)(2,1)S(1)}, bf16[16,8192]{1,0:T(8,128)(2,1)S(1)}, u32[]{:S(2)}, u32[]{:S(2)}) collective-permute-start(bf16[16,8192]{1,0:T(8,128)(2,1)S(1)} %fusion.103), channel_id=1, source_target_pairs={{16,0},{17,1},{18,2},{19,3},{20,4},{21,5},{22,6},{23,7},{24,8},{25... | collective-permute-start | bytes 786440 | tf_op jit(solution)/shard_map/while/body/eval_jaxpr/ppermute | solution.py:14
  236.7 0.7 copy-start.6
  242.2 9.9 %collective-permute-start.1 = (bf16[16,8192]{1,0:T(8,128)(2,1)S(1)}, bf16[16,8192]{1,0:T(8,128)(2,1)S(1)}, u32[]{:S(2)}, u32[]{:S(2)}) collective-permute-start(bf16[16,8192]{1,0:T(8,128)(2,1)S(1)} %fusion.103), channel_id=1, source_target_pairs={{16,0},{17,1},{18,2},{19,3},{20,4},{21,5},{22,6},{23,7},{24,8},{25... | collective-permute-start | bytes 786440 | tf_op jit(solution)/shard_map/while/body/eval_jaxpr/ppermute | solution.py:14
  252.1 0.7 copy-start.6
  257.6 9.1 %collective-permute-start.1 = (bf16[16,8192]{1,0:T(8,128)(2,1)S(1)}, bf16[16,8192]{1,0:T(8,128)(2,1)S(1)}, u32[]{:S(2)}, u32[]{:S(2)}) collective-permute-start(bf16[16,8192]{1,0:T(8,128)(2,1)S(1)} %fusion.103), channel_id=1, source_target_pairs={{16,0},{17,1},{18,2},{19,3},{20,4},{21,5},{22,6},{23,7},{24,8},{25... | collective-permute-start | bytes 786440 | tf_op jit(solution)/shard_map/while/body/eval_jaxpr/ppermute | solution.py:14
  266.6 0.7 copy-start.6
  272.1 8.3 %collective-permute-start.1 = (bf16[16,8192]{1,0:T(8,128)(2,1)S(1)}, bf16[16,8192]{1,0:T(8,128)(2,1)S(1)}, u32[]{:S(2)}, u32[]{:S(2)}) collective-permute-start(bf16[16,8192]{1,0:T(8,128)(2,1)S(1)} %fusion.103), channel_id=1, source_target_pairs={{16,0},{17,1},{18,2},{19,3},{20,4},{21,5},{22,6},{23,7},{24,8},{25... | collective-permute-start | bytes 786440 | tf_op jit(solution)/shard_map/while/body/eval_jaxpr/ppermute | solution.py:14
  280.3 0.7 copy-start.6
  285.8 8.3 %collective-permute-start.1 = (bf16[16,8192]{1,0:T(8,128)(2,1)S(1)}, bf16[16,8192]{1,0:T(8,128)(2,1)S(1)}, u32[]{:S(2)}, u32[]{:S(2)}) collective-permute-start(bf16[16,8192]{1,0:T(8,128)(2,1)S(1)} %fusion.103), channel_id=1, source_target_pairs={{16,0},{17,1},{18,2},{19,3},{20,4},{21,5},{22,6},{23,7},{24,8},{25... | collective-permute-start | bytes 786440 | tf_op jit(solution)/shard_map/while/body/eval_jaxpr/ppermute | solution.py:14
  294.1 0.7 copy-start.6
  299.5 8.3 %collective-permute-start.1 = (bf16[16,8192]{1,0:T(8,128)(2,1)S(1)}, bf16[16,8192]{1,0:T(8,128)(2,1)S(1)}, u32[]{:S(2)}, u32[]{:S(2)}) collective-permute-start(bf16[16,8192]{1,0:T(8,128)(2,1)S(1)} %fusion.103), channel_id=1, source_target_pairs={{16,0},{17,1},{18,2},{19,3},{20,4},{21,5},{22,6},{23,7},{24,8},{25... | collective-permute-start | bytes 786440 | tf_op jit(solution)/shard_map/while/body/eval_jaxpr/ppermute | solution.py:14
  307.8 0.7 copy-start.6
  313.2 8.3 %collective-permute-start.1 = (bf16[16,8192]{1,0:T(8,128)(2,1)S(1)}, bf16[16,8192]{1,0:T(8,128)(2,1)S(1)}, u32[]{:S(2)}, u32[]{:S(2)}) collective-permute-start(bf16[16,8192]{1,0:T(8,128)(2,1)S(1)} %fusion.103), channel_id=1, source_target_pairs={{16,0},{17,1},{18,2},{19,3},{20,4},{21,5},{22,6},{23,7},{24,8},{25... | collective-permute-start | bytes 786440 | tf_op jit(solution)/shard_map/while/body/eval_jaxpr/ppermute | solution.py:14
  321.5 0.7 copy-start.6
  322.2 2.2 copy-start.4
  322.2 2.5 copy-start.7
  326.3 3.0 copy-start.1
  329.3 4.2 copy-start.9
  329.3 4.2 copy-start.10
  411.6 4.9 copy-start.2
Sparse Core Ops, SparseCore 0:
  9.5 35.8 all-gather.3
  46.9 33.0 all-gather.5
  411.7 167.8 all-gather.7
